TPU v7x, 8 devices: a whole 2x2x1 slice. The times are simulated.
8 devices in a mesh: slab: 2 (over z, y), col: 2 (over x), row: 2 (over core).
Axes of the slice: x: 2, y: 2, z: 1, core: 2. Of those that a mesh axis runs over, the one named last changes fastest.
Arguments:
- tensor: bfloat16 [32, 256, 256, 256], P(None, 'row', 'col', 'slab')
- factor_one: float32 [256, 16], replicated
- factor_two: float32 [256, 16], replicated
- factor_three: float32 [256, 16], replicated
Outputs:
- output 1: float32 [32, 16, 16, 16], P(None, 'row', 'col', 'slab')
- output 2: float32 [32], replicated
All inputs are finite; a program needn't handle non-finite values.
Results may differ from a plain program's by a relative error of at most 0.001.
Values are sent between devices in bfloat16 or wider.
A program may use at most 1 GiB of HBM per device.

v0:
```python
import jax
import jax.numpy as jnp
from jax import lax
from jax.sharding import PartitionSpec as P


def solution(mesh):
    all_axes = ('row', 'col', 'slab')

    def local_part(x_block, f_one, f_two, f_three):
        snap_count, blk_one, blk_two, blk_three = x_block.shape
        rank_three = f_three.shape[1]
        part_three = jnp.dot(x_block.reshape(snap_count * blk_one * blk_two, blk_three), f_three.astype(jnp.bfloat16), preferred_element_type=jnp.float32)
        part_three = part_three.reshape(snap_count, blk_one, blk_two, rank_three)
        stage_a = lax.psum_scatter(part_three, 'slab', scatter_dimension=3, tiled=True).astype(jnp.bfloat16)
        part_two = jnp.einsum('tijc,jb->tibc', stage_a, f_two.astype(jnp.bfloat16), preferred_element_type=jnp.float32)
        stage_b = lax.psum_scatter(part_two, 'col', scatter_dimension=2, tiled=True).astype(jnp.bfloat16)
        part_one = jnp.einsum('tibc,ia->tabc', stage_b, f_one.astype(jnp.bfloat16), preferred_element_type=jnp.float32)
        core_block = lax.psum_scatter(part_one, 'row', scatter_dimension=1, tiled=True)
        x_energy = lax.psum(jnp.sum(jnp.square(x_block.astype(jnp.float32)), axis=(1, 2, 3)), all_axes)
        g_energy = lax.psum(jnp.sum(jnp.square(core_block), axis=(1, 2, 3)), all_axes)
        return core_block, (x_energy - g_energy) / x_energy

    return jax.shard_map(local_part, mesh=mesh, in_specs=(P(None, 'row', 'col', 'slab'), P('row', None), P('col', None), P('slab', None)), out_specs=(P(None, 'row', 'col', 'slab'), P()), check_vma=False)
```

profile of v0, /device:TPU:0, one launch (start us, length us, event | category | flops | bytes accessed | tf_op | source)
XLA Modules:
  0.0 613.8 jit_solution(7633150363018508975)
XLA Ops:
  7.2 0.0 copy-start
  7.2 0.0 reduce-scatter.7.cloned.1.call-start
  7.2 1.2 dynamic-slice.6
  9.1 0.0 copy-done
  9.1 57.9 %fusion.10 = f32[16,32,128,128]{3,0,2,1:T(8,128)} fusion(bf16[32,128,128,128]{3,2,1,0:T(8,128)(2,1)} %param.4, f32[256,16]{0,1:T(8,128)S(1)} %copy-done, s32[]{:T(128)} %bitcast), kind=kOutput, calls=%fused_computation.16 | convolution fusion | flops 2147483648 | bytes 167776256 | tf_op jit(solution)/shard_map/dot_general | solution.py:13
  67.0 27.5 %copy.30 = f32[16,32,128,128]{3,2,1,0:T(8,128)} copy(f32[16,32,128,128]{3,0,2,1:T(8,128)} %fusion.10) | data formatting | bytes 67108864 | tf_op jit(solution)/shard_map/dot_general | solution.py:13
  94.6 0.0 copy-start.3
  94.6 0.0 reduce-scatter.7.cloned.1.call-update
  94.6 0.0 copy-start.2
  94.6 0.0 reduce-scatter.11.cloned.1.call-start
  94.6 0.6 copy-done.3
  95.2 0.6 dynamic-slice.3
  96.4 367.2 %reduce-scatter.7.cloned.1.call-done = f32[32,128,128,8]{2,1,0,3:T(8,128)} async-done(((f32[32,128,128,16]{2,1,0,3:T(8,128)}), f32[32,128,128,8]{2,1,0,3:T(8,128)}) %reduce-scatter.7.cloned.1.call-update) | async-done | bytes 16777232 | tf_op jit(solution)/shard_map/reduce_scatter | solution.py:15
  463.7 8.1 %fusion.2 = f32[32,128,16,8]{1,2,3,0:T(8,128)S(1)} fusion(f32[256,16]{0,1:T(8,128)} %param.6, s32[]{:T(128)} %bitcast.4, f32[32,128,128,8]{2,1,0,3:T(8,128)} %reduce-scatter.7.cloned.1.call-done), kind=kOutput, calls=%fused_computation.5 | convolution fusion | flops 138412032 | bytes 18878976 | tf_op jit(solution)/shard_map/tijc,jb->tibc/dot_general | solution.py:16
  471.7 0.7 copy.14
  472.4 2.6 copy.31
  475.0 0.0 reduce-scatter.11.cloned.1.call-update
  475.0 0.0 reduce-scatter.9.cloned.1.call-start
  475.1 0.0 copy-done.2
  475.1 0.6 dynamic-slice
  476.3 27.9 %reduce-scatter.11.cloned.1.call-done = f32[8,32768]{1,0:T(8,128)} async-done(((f32[16,32768]{1,0:T(8,128)}), f32[8,32768]{1,0:T(8,128)}) %reduce-scatter.11.cloned.1.call-update) | async-done | bytes 1048592
  504.2 1.5 convolution_bitcast_fusion
  505.7 1.5 copy.7
  507.2 0.0 reduce-scatter.9.cloned.1.call-update
  507.3 0.0 copy-start.1
  507.3 76.1 %multiply_reduce_fusion = f32[32]{0:T(128)S(1)} fusion(bf16[32,128,128,128]{3,2,1,0:T(8,128)(2,1)} %param.4), kind=kLoop, calls=%fused_computation | loop fusion | flops 201326560 | bytes 134217856 | tf_op jit(solution)/shard_map/reduce_sum | solution.py:20
  583.4 0.0 reduce-scatter.9.cloned.1.call-done
  583.4 1.0 multiply_reduce_fusion.1
  584.5 22.3 %all-reduce = (f32[32]{0:T(128)S(1)}, f32[32]{0:T(128)S(1)}) all-reduce(f32[32]{0:T(128)S(1)} %multiply_reduce_fusion, f32[32]{0:T(128)S(1)} %multiply_reduce_fusion.1), channel_id=1, replica_groups=mesh['slab'=2,'col'=2,'row'=2] {'row','col','slab'}, use_global_device_ids=true, to_apply=%region_4.0 | all-reduce | flops 64 | bytes 512 | tf_op jit(solution)/shard_map/psum | solution.py:20
  606.7 0.5 subtract_divide_fusion
  607.2 0.0 copy-done.1
Async XLA Ops:
  7.2 2.0 copy-start
  7.2 456.5 %reduce-scatter.7.cloned.1.call-start = ((), (), s32[]{:S(2)}) async-start(), calls=%async_computation.3 | async-start | bytes 50331648 | tf_op jit(solution)/shard_map/reduce_scatter | solution.py:15
  94.6 0.7 copy-start.3
  94.6 380.5 %copy-start.2 = (u32[8]{0:T(128)S(1)}, u32[8]{0:T(128)}, u32[]{:S(2)}) copy-start(u32[8]{0:T(128)} %constant.2) | copy-start | bytes 100
  94.6 409.6 %reduce-scatter.11.cloned.1.call-start = ((), (), s32[]{:S(2)}) async-start(), calls=%async_computation.5 | async-start | bytes 3145728
  475.0 108.4 %reduce-scatter.9.cloned.1.call-start = ((), (), s32[]{:S(2)}) async-start(), calls=%async_computation.4 | async-start | bytes 786432 | tf_op jit(solution)/shard_map/reduce_scatter | solution.py:19
  507.3 100.0 %copy-start.1 = (f32[256,16]{0,1:T(8,128)S(1)}, f32[256,16]{0,1:T(8,128)}, u32[]{:S(2)}) copy-start(f32[256,16]{0,1:T(8,128)} %param.7) | copy-start | bytes 49156
Sparse Core Ops, SparseCore 0:
  94.7 368.9 reduce-scatter.6
  475.1 29.0 reduce-scatter.10
  507.4 5.1 reduce-scatter.8
where the time goes:
time: 614 us
  waiting for transfers between devices  395 us (64%)
  other arithmetic  77.7 us (13%)
  matrix products  67.4 us (11%)
  local copies, waits for them, and re-layouts  35.3 us (6%)
  blocking collectives  22.3 us (4%)
  between operations  15.8 us (3%)
    reduce_scatter x1, waiting for transfers between devices, local_part(): lax.psum_scatter(part_three, 'slab', scatter_dimension=3, tiled=True)  367 us
    reduce_sum x1, other arithmetic, local_part(): jnp.sum(jnp.square(x_block.astype(jnp.float32)), axis=(1, 2, 3))  76.1 us
    dot_general x1, matrix products, local_part(): jnp.dot(x_block.reshape(snap_count * blk_one * blk_two, blk_three), f_thr...  57.9 us
    unnamed x4, waiting for transfers between devices  27.9 us
    dot_general x1, local copies, waits for them, and re-layouts, local_part(): jnp.dot(x_block.reshape(snap_count * blk_one * blk_two, blk_three), f_thr...  27.5 us
    psum x1, blocking collectives, local_part(): lax.psum(jnp.sum(jnp.square(x_block.astype(jnp.float32)), axis=(1, 2, 3))...  22.3 us
  transfers between devices with their start and end apart: 3, of which 2 were waited for; matrix products, arithmetic and copies ran while one was open for 13% of the time, Pallas kernels for 0%

commit v1 on v0

v1 whole, which is shorter than its diff:
```python
import functools

import jax
import jax.numpy as jnp
from jax import lax
from jax.experimental import pallas as pl
from jax.experimental.pallas import tpu as pltpu
from jax.sharding import PartitionSpec as P

MESH = pl.DeviceIdType.MESH
F32, BF16 = jnp.float32, jnp.bfloat16
NT = (((1,), (1,)), ((), ()))

LAG = 4
RING = 2 * LAG
XBUF = 4
BRING = 4
SUB = 8


def other(axis):
    return {axis: 1 - lax.axis_index(axis)}


def offset_peer(dd):
    peer = {}
    for bit, axis in ((4, 'slab'), (2, 'col'), (1, 'row')):
        here = lax.axis_index(axis)
        peer[axis] = 1 - here if dd & bit else here
    return peer


def tree(parts):
    while len(parts) > 1:
        parts = [parts[k] + parts[k + 1] for k in range(0, len(parts), 2)]
    return parts[0]


def kernel(snaps, rows, x_hbm, f1_hbm, f2_hbm, f3_hbm, g_out, e_out,
           xbuf, f1, f2, f3, u3w, u2w, w1, own, ysend, yrecv, bown, xsend, xrecv,
           gpart, grecv, ex, exg, eg, x_sem, f_sem, ys_sem, yr_sem, xs_sem, xr_sem, g_sem, ex_ssem, ex_rsem, eg_ssem, eg_rsem):
    nq = 128 // rows
    nc = snaps * nq
    width = rows * 8
    slab, col, row = (lax.axis_index(a) for a in ('slab', 'col', 'row'))

    def x_copy(c):
        slot = lax.rem(c, XBUF)
        return pltpu.make_async_copy(x_hbm.at[c], xbuf.at[slot], x_sem.at[slot])

    f_copies = [pltpu.make_async_copy(src, dst, f_sem.at[k]) for k, (src, dst) in enumerate(((f3_hbm, f3), (f2_hbm, f2), (f1_hbm, f1)))]
    f_copies[0].start()
    for c in range(XBUF):
        x_copy(c).start()
    f_copies[1].start()
    f_copies[2].start()

    barrier = pltpu.get_barrier_semaphore()
    for dd in range(1, 8):
        pl.semaphore_signal(barrier, inc=1, device_id=offset_peer(dd), device_id_type=MESH)

    def swapped(block, flip):
        return jnp.where(flip == 0, block, jnp.concatenate([block[8:], block[:8]], axis=0)).astype(BF16)

    f_copies[0].wait()
    u3w[...] = swapped(f3[:, pl.ds(pl.multiple_of(slab * 128, 128), 128)], slab)
    ex[...] = jnp.zeros_like(ex)
    pl.semaphore_wait(barrier, 7)

    def y_copy(c):
        slot = lax.rem(c, RING)
        return pltpu.make_async_remote_copy(ysend.at[slot], yrecv.at[slot], ys_sem.at[slot], yr_sem.at[slot], device_id=other('slab'), device_id_type=MESH)

    def b_copy(c):
        slot = lax.rem(c, BRING)
        return pltpu.make_async_remote_copy(xsend.at[slot], xrecv.at[slot], xs_sem.at[slot], xr_sem.at[slot], device_id=other('col'), device_id_type=MESH)

    def ex_copy(dd):
        return pltpu.make_async_remote_copy(exg.at[0], exg.at[dd], ex_ssem.at[dd], ex_rsem.at[dd], device_id=offset_peer(dd), device_id_type=MESH)

    def eg_copy(dd):
        return pltpu.make_async_remote_copy(eg.at[0], eg.at[dd // 2], eg_ssem.at[dd // 2], eg_rsem.at[dd // 2], device_id=offset_peer(dd), device_id_type=MESH)

    g_copy = pltpu.make_async_remote_copy(gpart, grecv, g_sem.at[0], g_sem.at[1], device_id=other('row'), device_id_type=MESH)

    def mode_three(c):
        slot, xs = lax.rem(c, RING), lax.rem(c, XBUF)
        x_copy(c).wait()

        @pl.when(c >= RING)
        def _():
            y_copy(c).wait_send()

        def block(k, acc):
            x = xbuf[xs, pl.ds(pl.multiple_of(k * SUB * 128, SUB * 128), SUB * 128), :]
            part = lax.dot_general(u3w[...], x, NT, preferred_element_type=F32)
            for i in range(SUB):
                own[slot, k * SUB + i] = part[:8, i * 128:(i + 1) * 128]
                ysend[slot, k * SUB + i] = part[8:, i * 128:(i + 1) * 128]
            xf = x.astype(F32).reshape(-1, 4, 8, 128)
            return acc + jnp.sum(xf * xf, axis=0)

        acc = lax.fori_loop(0, rows // SUB, block, jnp.zeros((4, 8, 128), F32))
        t = lax.div(c, nq)
        ex[t] += jnp.sum(acc, axis=0)

        @pl.when(c + XBUF < nc)
        def _():
            x_copy(c + XBUF).start()

    def mode_two(c):
        slot, bslot = lax.rem(c, RING), lax.rem(c, BRING)
        y_copy(c).wait_recv()

        @pl.when(c >= BRING)
        def _():
            b_copy(c).wait_send()

        a = (own[slot] + yrecv[slot]).reshape(width, 128).astype(BF16)
        part = lax.dot_general(u2w[...], a, NT, preferred_element_type=F32)
        bown[bslot] = part[:8]
        xsend[bslot] = part[8:]

    def mode_one(c):
        bslot = lax.rem(c, BRING)
        b_copy(c).wait_recv()
        b = (bown[bslot] + xrecv[bslot]).astype(BF16)
        q, t = lax.rem(c, nq), lax.div(c, nq)
        g = jnp.dot(b, w1[q], preferred_element_type=F32)

        @pl.when(q == 0)
        def _():
            gpart[t] = g

        @pl.when(q > 0)
        def _():
            gpart[t] += g

    def late_setup():
        f_copies[1].wait()
        f_copies[2].wait()
        u2w[...] = swapped(f2[:, pl.ds(pl.multiple_of(col * 128, 128), 128)], col)
        u1 = f1[:, pl.ds(pl.multiple_of(row * 128, 128), 128)].astype(BF16)
        spread = (lax.broadcasted_iota(jnp.int32, (16, 128), 1) // 8 == lax.broadcasted_iota(jnp.int32, (16, 128), 0)).astype(BF16)
        r = lax.broadcasted_iota(jnp.int32, (width, 128), 0)
        l = lax.broadcasted_iota(jnp.int32, (width, 128), 1)
        for q in range(nq):
            pick = (l == q * rows + r // 8).astype(BF16)
            rowed = lax.dot_general(pick, u1, NT, preferred_element_type=F32).astype(BF16)
            wide = jnp.dot(rowed, spread, preferred_element_type=F32)
            w1[q] = jnp.where(r % 8 == l % 8, wide, 0.0).astype(BF16)

    def step(s, carry):
        @pl.when((s >= 1) & (s <= nc))
        def _():
            y_copy(s - 1).start()

        @pl.when(s >= LAG + 1)
        def _():
            b_copy(s - LAG - 1).start()

        @pl.when(s < nc)
        def _():
            mode_three(s)

        @pl.when(s == 2)
        def _():
            late_setup()

        @pl.when(s == nc)
        def _():
            exg[0] = jnp.broadcast_to(jnp.sum(jnp.sum(ex[...], axis=1), axis=1, keepdims=True), (snaps, 128))

        @pl.when(s == nc + 1)
        def _():
            for dd in range(1, 8):
                ex_copy(dd).start()

        @pl.when((s >= LAG) & (s < nc + LAG))
        def _():
            mode_two(s - LAG)

        @pl.when(s >= LAG + 1)
        def _():
            mode_one(s - LAG - 1)

        return carry

    lax.fori_loop(0, nc + LAG + 1, step, 0)

    g_copy.start()
    for c in range(nc - RING, nc):
        y_copy(c).wait_send()
    for c in range(nc - BRING, nc):
        b_copy(c).wait_send()
    for dd in range(1, 8):
        ex_copy(dd).wait()
    x_energy = tree([exg[dd] for dd in range(8)])
    g_copy.wait()

    g = gpart[...] + grecv[...]
    eg[0] = jnp.broadcast_to(jnp.sum(jnp.sum(g * g, axis=1), axis=1, keepdims=True), (snaps, 128))
    for dd in (2, 4, 6):
        eg_copy(dd).start()
    for b in range(8):
        turned = g[:, b, :].T
        g_out[:, b] = jnp.where(row == 0, turned[:64], turned[64:]).reshape(8, 8, snaps)
    for dd in (2, 4, 6):
        eg_copy(dd).wait()
    g_energy = tree([eg[k] for k in range(4)])
    rel = (x_energy - g_energy) / x_energy
    diag = lax.broadcasted_iota(jnp.int32, (snaps, 128), 0) == lax.broadcasted_iota(jnp.int32, (snaps, 128), 1)
    e_out[...] = jnp.sum(jnp.where(diag, rel, 0.0), axis=0, keepdims=True)[:, :snaps]


def solution(mesh):
    rows = 32

    def local_part(x_block, f_one, f_two, f_three):
        snaps = x_block.shape[0]
        nq = 128 // rows
        nc = snaps * nq
        dma = pltpu.SemaphoreType.DMA
        hbm = pl.BlockSpec(memory_space=pl.ANY)
        vmem = pl.BlockSpec(memory_space=pltpu.VMEM)
        g, e = pl.pallas_call(
            functools.partial(kernel, snaps, rows),
            out_shape=(jax.ShapeDtypeStruct((8, 8, 8, snaps), F32), jax.ShapeDtypeStruct((1, snaps), F32)),
            in_specs=[hbm] * 4,
            out_specs=(vmem, vmem),
            scratch_shapes=[
                pltpu.VMEM((XBUF, rows * 128, 128), BF16),
                pltpu.VMEM((16, 256), F32), pltpu.VMEM((16, 256), F32), pltpu.VMEM((16, 256), F32),
                pltpu.VMEM((16, 128), BF16), pltpu.VMEM((16, 128), BF16),
                pltpu.VMEM((nq, rows * 8, 128), BF16),
                pltpu.VMEM((RING, rows, 8, 128), F32), pltpu.VMEM((RING, rows, 8, 128), F32), pltpu.VMEM((RING, rows, 8, 128), F32),
                pltpu.VMEM((BRING, 8, rows * 8), F32), pltpu.VMEM((BRING, 8, rows * 8), F32), pltpu.VMEM((BRING, 8, rows * 8), F32),
                pltpu.VMEM((snaps, 8, 128), F32), pltpu.VMEM((snaps, 8, 128), F32),
                pltpu.VMEM((snaps, 8, 128), F32), pltpu.VMEM((8, snaps, 128), F32), pltpu.VMEM((4, snaps, 128), F32),
                dma((XBUF,)), dma((3,)), dma((RING,)), dma((RING,)), dma((BRING,)), dma((BRING,)), dma((2,)), dma((8,)), dma((8,)), dma((4,)), dma((4,)),
            ],
            compiler_params=pltpu.CompilerParams(collective_id=0, has_side_effects=True),
        )(x_block.reshape(nc, rows * 128, 128), f_one.T, f_two.T, f_three.T)
        return g.transpose(3, 0, 1, 2), e.reshape(snaps)

    return jax.shard_map(local_part, mesh=mesh, in_specs=(P(None, 'row', 'col', 'slab'), P(None, None), P(None, None), P(None, None)), out_specs=(P(None, 'row', 'col', 'slab'), P()), check_vma=False)
```

time: 614 us -> 380 us (0.62)
  waiting for transfers between devices: 395 us -> 0 us
  Pallas kernels: 0 us -> 376 us
  other arithmetic: 77.7 us -> 0 us
  matrix products: 67.4 us -> 0 us
  local copies, waits for them, and re-layouts: 35.3 us -> 2.8 us
  blocking collectives: 22.3 us -> 0 us
  between operations: 15.8 us -> 0.64 us
    pallas_call x0 -> x1, Pallas kernels: none -> 376 us  [local_part(): pl.pallas_call(functools.partial(kernel, snaps, rows), out_shape=(jax.Sha...]
    reduce_scatter x2 -> x0, waiting for transfers between devices: 367 us -> none  [the longest x1 367 us: local_part(): lax.psum_scatter(part_three, 'slab', scatter_dimension=3, tiled=True)]
    reduce_sum x2 -> x0, other arithmetic: 77.2 us -> none  [the longest x1 76.1 us: local_part(): jnp.sum(jnp.square(x_block.astype(jnp.float32)), axis=(1, 2, 3))]
    dot_general x3 -> x0, matrix products: 67.4 us -> none  [the longest x1 57.9 us: local_part(): jnp.dot(x_block.reshape(snap_count * blk_one * blk_two, blk_three), f_thr...]
    unnamed x4 -> x0, waiting for transfers between devices: 27.9 us -> none
    dot_general x1 -> x0, local copies, waits for them, and re-layouts: 27.5 us -> none  [local_part(): jnp.dot(x_block.reshape(snap_count * blk_one * blk_two, blk_three), f_thr...]
    psum x1 -> x0, blocking collectives: 22.3 us -> none  [local_part(): lax.psum(jnp.sum(jnp.square(x_block.astype(jnp.float32)), axis=(1, 2, 3))...]
  transfers between devices with their start and end apart: 3 -> 0, of which waited for: 2 -> 0; matrix products, arithmetic and copies ran while one was open for 13% -> 0% of each run, Pallas kernels for 0% -> 0%
where the time goes in v1:
time: 380 us
  Pallas kernels  376 us (99%)
    pallas_call x1, Pallas kernels, local_part(): pl.pallas_call(functools.partial(kernel, snaps, rows), out_shape=(jax.Sha...  376 us

profile of v1, /device:TPU:0, one launch (start us, length us, event | category | flops | bytes accessed | tf_op | source)
XLA Modules:
  0.0 379.9 jit_solution(4567694300698610861)
XLA Ops:
  0.6 376.5 %shard_map.59 = (f32[8,8,8,32]{3,2,1,0:T(8,128)}, f32[1,32]{1,0:T(1,128)}) custom-call(bf16[128,4096,128]{2,1,0:T(8,128)(2,1)} %bitcast.x_hbm, f32[16,256]{1,0:T(8,128)} %bitcast.7, f32[16,256]{1,0:T(8,128)} %bitcast.8, f32[16,256]{1,0:T(8,128)} %bitcast.9), custom_call_target="tpu_custom_call" | custom-call | tf_op jit(solution)/shard_map/pallas_call | solution.py:226
  377.1 1.7 copy.8
  378.8 1.1 copy.9

commit v2 on v1

--- a/solution.py
+++ b/solution.py
@@ -38,10 +38,11 @@
 
 def kernel(snaps, rows, x_hbm, f1_hbm, f2_hbm, f3_hbm, g_out, e_out,
            xbuf, f1, f2, f3, u3w, u2w, w1, own, ysend, yrecv, bown, xsend, xrecv,
-           gpart, grecv, ex, exg, eg, x_sem, f_sem, ys_sem, yr_sem, xs_sem, xr_sem, g_sem, ex_ssem, ex_rsem, eg_ssem, eg_rsem):
+           gpart, grecv, ex, energy, glast, x_sem, f_sem, ys_sem, yr_sem, xs_sem, xr_sem, g_sem, en_ssem, en_rsem, gl_ssem, gl_rsem):
     nq = 128 // rows
     nc = snaps * nq
     width = rows * 8
+    last = snaps - 1
     slab, col, row = (lax.axis_index(a) for a in ('slab', 'col', 'row'))
 
     def x_copy(c):
@@ -50,13 +51,10 @@
 
     f_copies = [pltpu.make_async_copy(src, dst, f_sem.at[k]) for k, (src, dst) in enumerate(((f3_hbm, f3), (f2_hbm, f2), (f1_hbm, f1)))]
     f_copies[0].start()
-    for c in range(XBUF):
-        x_copy(c).start()
-    f_copies[1].start()
-    f_copies[2].start()
+    x_copy(0).start()
 
     barrier = pltpu.get_barrier_semaphore()
-    for dd in range(1, 8):
+    for dd in (4, 2, 1):
         pl.semaphore_signal(barrier, inc=1, device_id=offset_peer(dd), device_id_type=MESH)
 
     def swapped(block, flip):
@@ -65,7 +63,6 @@
     f_copies[0].wait()
     u3w[...] = swapped(f3[:, pl.ds(pl.multiple_of(slab * 128, 128), 128)], slab)
     ex[...] = jnp.zeros_like(ex)
-    pl.semaphore_wait(barrier, 7)
 
     def y_copy(c):
         slot = lax.rem(c, RING)
@@ -75,13 +72,14 @@
         slot = lax.rem(c, BRING)
         return pltpu.make_async_remote_copy(xsend.at[slot], xrecv.at[slot], xs_sem.at[slot], xr_sem.at[slot], device_id=other('col'), device_id_type=MESH)
 
-    def ex_copy(dd):
-        return pltpu.make_async_remote_copy(exg.at[0], exg.at[dd], ex_ssem.at[dd], ex_rsem.at[dd], device_id=offset_peer(dd), device_id_type=MESH)
-
-    def eg_copy(dd):
-        return pltpu.make_async_remote_copy(eg.at[0], eg.at[dd // 2], eg_ssem.at[dd // 2], eg_rsem.at[dd // 2], device_id=offset_peer(dd), device_id_type=MESH)
-
-    g_copy = pltpu.make_async_remote_copy(gpart, grecv, g_sem.at[0], g_sem.at[1], device_id=other('row'), device_id_type=MESH)
+    def energy_copy(dd):
+        return pltpu.make_async_remote_copy(energy.at[0], energy.at[dd], en_ssem.at[dd], en_rsem.at[dd], device_id=offset_peer(dd), device_id_type=MESH)
+
+    def last_copy(dd):
+        return pltpu.make_async_remote_copy(gpart.at[last], glast.at[dd], gl_ssem.at[dd], gl_rsem.at[dd], device_id=offset_peer(dd), device_id_type=MESH)
+
+    early = pl.ds(0, last)
+    g_copy = pltpu.make_async_remote_copy(gpart.at[early], grecv.at[early], g_sem.at[0], g_sem.at[1], device_id=other('row'), device_id_type=MESH)
 
     def mode_three(c):
         slot, xs = lax.rem(c, RING), lax.rem(c, XBUF)
@@ -120,6 +118,7 @@
         part = lax.dot_general(u2w[...], a, NT, preferred_element_type=F32)
         bown[bslot] = part[:8]
         xsend[bslot] = part[8:]
+        b_copy(c).start()
 
     def mode_one(c):
         bslot = lax.rem(c, BRING)
@@ -150,67 +149,95 @@
             wide = jnp.dot(rowed, spread, preferred_element_type=F32)
             w1[q] = jnp.where(r % 8 == l % 8, wide, 0.0).astype(BF16)
 
+    def as_row(column, count):
+        i = lax.broadcasted_iota(jnp.int32, (count, 128), 0)
+        return jnp.sum(jnp.where(i == lax.broadcasted_iota(jnp.int32, (count, 128), 1), column, 0.0), axis=0, keepdims=True)
+
+    def row_sums(blocks):
+        return as_row(jnp.sum(jnp.sum(blocks, axis=1), axis=1, keepdims=True), blocks.shape[0])
+
     def step(s, carry):
-        @pl.when((s >= 1) & (s <= nc))
+        @pl.when((s >= 2) & (s <= nc))
         def _():
             y_copy(s - 1).start()
 
+        @pl.when(s < nc)
+        def _():
+            mode_three(s)
+
+        @pl.when(s == 2)
+        def _():
+            late_setup()
+
+        @pl.when(s == nc)
+        def _():
+            energy[0, :1] = row_sums(ex[...])
+
+        @pl.when(s == nc + LAG - 3)
+        def _():
+            g_copy.start()
+
+        @pl.when((s >= LAG) & (s < nc + LAG))
+        def _():
+            mode_two(s - LAG)
+
+        @pl.when(s == nc + LAG - 2)
+        def _():
+            g_copy.wait()
+            g = gpart[early] + grecv[early]
+            grecv[early] = g
+            energy[0, 1:] = row_sums(g * g)
+
+        @pl.when(s == nc + LAG - 1)
+        def _():
+            for dd in range(1, 8):
+                energy_copy(dd).start()
+
         @pl.when(s >= LAG + 1)
         def _():
-            b_copy(s - LAG - 1).start()
-
-        @pl.when(s < nc)
-        def _():
-            mode_three(s)
-
-        @pl.when(s == 2)
-        def _():
-            late_setup()
-
-        @pl.when(s == nc)
-        def _():
-            exg[0] = jnp.broadcast_to(jnp.sum(jnp.sum(ex[...], axis=1), axis=1, keepdims=True), (snaps, 128))
-
-        @pl.when(s == nc + 1)
-        def _():
-            for dd in range(1, 8):
-                ex_copy(dd).start()
-
-        @pl.when((s >= LAG) & (s < nc + LAG))
-        def _():
-            mode_two(s - LAG)
-
-        @pl.when(s >= LAG + 1)
-        def _():
             mode_one(s - LAG - 1)
 
         return carry
 
-    lax.fori_loop(0, nc + LAG + 1, step, 0)
-
-    g_copy.start()
+    mode_three(0)
+    pl.semaphore_wait(barrier, 3)
+    y_copy(0).start()
+    for c in range(1, XBUF):
+        x_copy(c).start()
+    f_copies[1].start()
+    f_copies[2].start()
+    lax.fori_loop(1, nc + LAG + 1, step, 0)
+
+    for dd in (6, 7, 4, 5, 2, 3, 1):
+        last_copy(dd).start()
     for c in range(nc - RING, nc):
         y_copy(c).wait_send()
     for c in range(nc - BRING, nc):
         b_copy(c).wait_send()
+    last_copy(1).wait()
+    mine = gpart[last] + glast[1]
+    grecv[last] = mine
+    for b in range(8):
+        turned = grecv[:, b, :].T
+        g_out[:, b] = jnp.where(row == 0, turned[:64], turned[64:]).reshape(8, 8, snaps)
     for dd in range(1, 8):
-        ex_copy(dd).wait()
-    x_energy = tree([exg[dd] for dd in range(8)])
-    g_copy.wait()
-
-    g = gpart[...] + grecv[...]
-    eg[0] = jnp.broadcast_to(jnp.sum(jnp.sum(g * g, axis=1), axis=1, keepdims=True), (snaps, 128))
-    for dd in (2, 4, 6):
-        eg_copy(dd).start()
-    for b in range(8):
-        turned = g[:, b, :].T
-        g_out[:, b] = jnp.where(row == 0, turned[:64], turned[64:]).reshape(8, 8, snaps)
-    for dd in (2, 4, 6):
-        eg_copy(dd).wait()
-    g_energy = tree([eg[k] for k in range(4)])
-    rel = (x_energy - g_energy) / x_energy
-    diag = lax.broadcasted_iota(jnp.int32, (snaps, 128), 0) == lax.broadcasted_iota(jnp.int32, (snaps, 128), 1)
-    e_out[...] = jnp.sum(jnp.where(diag, rel, 0.0), axis=0, keepdims=True)[:, :snaps]
+        energy_copy(dd).wait()
+    x_energy = tree([energy[dd, :1] for dd in range(8)])
+    g_energy = tree([energy[dd, 1:] for dd in (0, 2, 4, 6)])
+    for dd in range(2, 8):
+        last_copy(dd).wait()
+    chips = [mine] + [glast[dd] + glast[dd + 1] for dd in (2, 4, 6)]
+    final = jnp.sum(tree([g * g for g in chips]))
+    g_energy = jnp.where(lax.broadcasted_iota(jnp.int32, (1, 128), 1) == last, final, g_energy)
+    e_out[...] = ((x_energy - g_energy) / x_energy)[:, :snaps]
+
+
+def finish(g_in, e_in, g_out, e_out, sem):
+    copies = [pltpu.make_async_copy(g_in, g_out, sem.at[0]), pltpu.make_async_copy(e_in, e_out, sem.at[1])]
+    for copy in copies:
+        copy.start()
+    for copy in copies:
+        copy.wait()
 
 
 def solution(mesh):
@@ -221,11 +248,11 @@
         nq = 128 // rows
         nc = snaps * nq
         dma = pltpu.SemaphoreType.DMA
-        hbm = pl.BlockSpec(memory_space=pl.ANY)
+        hbm = pl.BlockSpec(memory_space=pltpu.HBM)
         vmem = pl.BlockSpec(memory_space=pltpu.VMEM)
         g, e = pl.pallas_call(
             functools.partial(kernel, snaps, rows),
-            out_shape=(jax.ShapeDtypeStruct((8, 8, 8, snaps), F32), jax.ShapeDtypeStruct((1, snaps), F32)),
+            out_shape=(pltpu.VMEM((8, 8, 8, snaps), F32), pltpu.VMEM((1, snaps), F32)),
             in_specs=[hbm] * 4,
             out_specs=(vmem, vmem),
             scratch_shapes=[
@@ -236,11 +263,19 @@
                 pltpu.VMEM((RING, rows, 8, 128), F32), pltpu.VMEM((RING, rows, 8, 128), F32), pltpu.VMEM((RING, rows, 8, 128), F32),
                 pltpu.VMEM((BRING, 8, rows * 8), F32), pltpu.VMEM((BRING, 8, rows * 8), F32), pltpu.VMEM((BRING, 8, rows * 8), F32),
                 pltpu.VMEM((snaps, 8, 128), F32), pltpu.VMEM((snaps, 8, 128), F32),
-                pltpu.VMEM((snaps, 8, 128), F32), pltpu.VMEM((8, snaps, 128), F32), pltpu.VMEM((4, snaps, 128), F32),
-                dma((XBUF,)), dma((3,)), dma((RING,)), dma((RING,)), dma((BRING,)), dma((BRING,)), dma((2,)), dma((8,)), dma((8,)), dma((4,)), dma((4,)),
+                pltpu.VMEM((snaps, 8, 128), F32), pltpu.VMEM((8, 2, 128), F32), pltpu.VMEM((8, 8, 128), F32),
+                dma((XBUF,)), dma((3,)), dma((RING,)), dma((RING,)), dma((BRING,)), dma((BRING,)), dma((2,)), dma((8,)), dma((8,)), dma((8,)), dma((8,)),
             ],
-            compiler_params=pltpu.CompilerParams(collective_id=0, has_side_effects=True),
-        )(x_block.reshape(nc, rows * 128, 128), f_one.T, f_two.T, f_three.T)
+            compiler_params=pltpu.CompilerParams(collective_id=0, has_side_effects=True, vmem_limit_bytes=40 * 1024 * 1024),
+        )(x_block.reshape(nc, rows * 128, 128), *(pltpu.with_memory_space_constraint(f.T, pltpu.HBM) for f in (f_one, f_two, f_three)))
+        g, e = pl.pallas_call(
+            finish,
+            out_shape=(jax.ShapeDtypeStruct((8, 8, 8, snaps), F32), jax.ShapeDtypeStruct((1, snaps), F32)),
+            in_specs=[vmem] * 2,
+            out_specs=(hbm, hbm),
+            scratch_shapes=[dma((2,))],
+            compiler_params=pltpu.CompilerParams(vmem_limit_bytes=4 * 1024 * 1024),
+        )(*(pltpu.with_memory_space_constraint(r, pltpu.VMEM) for r in (g, e)))
         return g.transpose(3, 0, 1, 2), e.reshape(snaps)
 
     return jax.shard_map(local_part, mesh=mesh, in_specs=(P(None, 'row', 'col', 'slab'), P(None, None), P(None, None), P(None, None)), out_specs=(P(None, 'row', 'col', 'slab'), P()), check_vma=False)

time: 380 us -> 373 us (0.982)
    pallas_call x1 -> x2, Pallas kernels: 376 us -> 373 us  [the longest x1 372 us: local_part(): pl.pallas_call(functools.partial(kernel, snaps, rows), out_shape=(pltpu.V...]
where the time goes in v2:
time: 373 us
  Pallas kernels  373 us (100%)
    pallas_call x1, Pallas kernels, local_part(): pl.pallas_call(functools.partial(kernel, snaps, rows), out_shape=(pltpu.V...  372 us

profile of v2, /device:TPU:0, one launch (start us, length us, event | category | flops | bytes accessed | tf_op | source)
XLA Modules:
  0.0 373.3 jit_solution(11355087536435891125)
XLA Ops:
  0.6 371.9 %shard_map.59 = (f32[8,8,8,32]{3,2,1,0:T(8,128)S(1)}, f32[1,32]{1,0:T(1,128)S(1)}) custom-call(bf16[128,4096,128]{2,1,0:T(8,128)(2,1)} %bitcast.x_hbm, f32[16,256]{1,0:T(8,128)} %bitcast.6, f32[16,256]{1,0:T(8,128)} %bitcast.7, f32[16,256]{1,0:T(8,128)} %bitcast.8), custom_call_target="tpu_custom_call" | custom-call | tf_op jit(solution)/shard_map/pallas_call | solution.py:253
  372.5 0.7 shard_map.60

commit v3 on v2

--- a/solution.py
+++ b/solution.py
@@ -38,7 +38,7 @@
 
 def kernel(snaps, rows, x_hbm, f1_hbm, f2_hbm, f3_hbm, g_out, e_out,
            xbuf, f1, f2, f3, u3w, u2w, w1, own, ysend, yrecv, bown, xsend, xrecv,
-           gpart, grecv, ex, energy, glast, x_sem, f_sem, ys_sem, yr_sem, xs_sem, xr_sem, g_sem, en_ssem, en_rsem, gl_ssem, gl_rsem):
+           gpart, grecv, ex, energy, glast, u2n, w1o, blast, x_sem, f_sem, ys_sem, yr_sem, xs_sem, xr_sem, g_sem, en_ssem, en_rsem, gl_ssem, gl_rsem, bl_ssem, bl_rsem, x0_sem):
     nq = 128 // rows
     nc = snaps * nq
     width = rows * 8
@@ -50,8 +50,12 @@
         return pltpu.make_async_copy(x_hbm.at[c], xbuf.at[slot], x_sem.at[slot])
 
     f_copies = [pltpu.make_async_copy(src, dst, f_sem.at[k]) for k, (src, dst) in enumerate(((f3_hbm, f3), (f2_hbm, f2), (f1_hbm, f1)))]
+    pieces = rows // SUB
+    x_first = [pltpu.make_async_copy(x_hbm.at[0, pl.ds(k * SUB * 128, SUB * 128)], xbuf.at[0, pl.ds(k * SUB * 128, SUB * 128)], x0_sem.at[k]) for k in range(pieces)]
+    x_first[0].start()
     f_copies[0].start()
-    x_copy(0).start()
+    for copy in x_first[1:]:
+        copy.start()
 
     barrier = pltpu.get_barrier_semaphore()
     for dd in (4, 2, 1):
@@ -72,6 +76,13 @@
         slot = lax.rem(c, BRING)
         return pltpu.make_async_remote_copy(xsend.at[slot], xrecv.at[slot], xs_sem.at[slot], xr_sem.at[slot], device_id=other('col'), device_id_type=MESH)
 
+    def y_first(k):
+        part = pl.ds(k * SUB, SUB)
+        return pltpu.make_async_remote_copy(ysend.at[0, part], yrecv.at[0, part], ys_sem.at[0], yr_sem.at[0], device_id=other('slab'), device_id_type=MESH)
+
+    def wide_copy(dd):
+        return pltpu.make_async_remote_copy(blast.at[0], blast.at[dd], bl_ssem.at[dd], bl_rsem.at[dd], device_id=offset_peer(dd), device_id_type=MESH)
+
     def energy_copy(dd):
         return pltpu.make_async_remote_copy(energy.at[0], energy.at[dd], en_ssem.at[dd], en_rsem.at[dd], device_id=offset_peer(dd), device_id_type=MESH)
 
@@ -80,6 +91,15 @@
 
     early = pl.ds(0, last)
     g_copy = pltpu.make_async_remote_copy(gpart.at[early], grecv.at[early], g_sem.at[0], g_sem.at[1], device_id=other('row'), device_id_type=MESH)
+
+    def block(slot, xs, k):
+        x = xbuf[xs, pl.ds(pl.multiple_of(k * SUB * 128, SUB * 128), SUB * 128), :]
+        part = lax.dot_general(u3w[...], x, NT, preferred_element_type=F32)
+        for i in range(SUB):
+            own[slot, k * SUB + i] = part[:8, i * 128:(i + 1) * 128]
+            ysend[slot, k * SUB + i] = part[8:, i * 128:(i + 1) * 128]
+        xf = x.astype(F32).reshape(-1, 4, 8, 128)
+        return jnp.sum(xf * xf, axis=0)
 
     def mode_three(c):
         slot, xs = lax.rem(c, RING), lax.rem(c, XBUF)
@@ -89,16 +109,7 @@
         def _():
             y_copy(c).wait_send()
 
-        def block(k, acc):
-            x = xbuf[xs, pl.ds(pl.multiple_of(k * SUB * 128, SUB * 128), SUB * 128), :]
-            part = lax.dot_general(u3w[...], x, NT, preferred_element_type=F32)
-            for i in range(SUB):
-                own[slot, k * SUB + i] = part[:8, i * 128:(i + 1) * 128]
-                ysend[slot, k * SUB + i] = part[8:, i * 128:(i + 1) * 128]
-            xf = x.astype(F32).reshape(-1, 4, 8, 128)
-            return acc + jnp.sum(xf * xf, axis=0)
-
-        acc = lax.fori_loop(0, rows // SUB, block, jnp.zeros((4, 8, 128), F32))
+        acc = lax.fori_loop(0, pieces, lambda k, acc: acc + block(slot, xs, k), jnp.zeros((4, 8, 128), F32))
         t = lax.div(c, nq)
         ex[t] += jnp.sum(acc, axis=0)
 
@@ -106,16 +117,19 @@
         def _():
             x_copy(c + XBUF).start()
 
+    def mode_two_rows(c):
+        slot = lax.rem(c, RING)
+        y_copy(c).wait_recv()
+        return (own[slot] + yrecv[slot]).reshape(width, 128).astype(BF16)
+
     def mode_two(c):
-        slot, bslot = lax.rem(c, RING), lax.rem(c, BRING)
-        y_copy(c).wait_recv()
+        bslot = lax.rem(c, BRING)
 
         @pl.when(c >= BRING)
         def _():
             b_copy(c).wait_send()
 
-        a = (own[slot] + yrecv[slot]).reshape(width, 128).astype(BF16)
-        part = lax.dot_general(u2w[...], a, NT, preferred_element_type=F32)
+        part = lax.dot_general(u2w[...], mode_two_rows(c), NT, preferred_element_type=F32)
         bown[bslot] = part[:8]
         xsend[bslot] = part[8:]
         b_copy(c).start()
@@ -138,16 +152,23 @@
     def late_setup():
         f_copies[1].wait()
         f_copies[2].wait()
-        u2w[...] = swapped(f2[:, pl.ds(pl.multiple_of(col * 128, 128), 128)], col)
-        u1 = f1[:, pl.ds(pl.multiple_of(row * 128, 128), 128)].astype(BF16)
+        block_two = f2[:, pl.ds(pl.multiple_of(col * 128, 128), 128)]
+        u2n[...] = block_two.astype(BF16)
+        u2w[...] = swapped(block_two, col)
         spread = (lax.broadcasted_iota(jnp.int32, (16, 128), 1) // 8 == lax.broadcasted_iota(jnp.int32, (16, 128), 0)).astype(BF16)
         r = lax.broadcasted_iota(jnp.int32, (width, 128), 0)
         l = lax.broadcasted_iota(jnp.int32, (width, 128), 1)
-        for q in range(nq):
+
+        def diagonal(which, q):
+            u1 = f1[:, pl.ds(pl.multiple_of(which * 128, 128), 128)].astype(BF16)
             pick = (l == q * rows + r // 8).astype(BF16)
             rowed = lax.dot_general(pick, u1, NT, preferred_element_type=F32).astype(BF16)
             wide = jnp.dot(rowed, spread, preferred_element_type=F32)
-            w1[q] = jnp.where(r % 8 == l % 8, wide, 0.0).astype(BF16)
+            return jnp.where(r % 8 == l % 8, wide, 0.0).astype(BF16)
+
+        for q in range(nq):
+            w1[q] = diagonal(row, q)
+        w1o[...] = diagonal(1 - row, nq - 1)
 
     def as_row(column, count):
         i = lax.broadcasted_iota(jnp.int32, (count, 128), 0)
@@ -177,7 +198,7 @@
         def _():
             g_copy.start()
 
-        @pl.when((s >= LAG) & (s < nc + LAG))
+        @pl.when(s >= LAG)
         def _():
             mode_two(s - LAG)
 
@@ -188,34 +209,54 @@
             grecv[early] = g
             energy[0, 1:] = row_sums(g * g)
 
-        @pl.when(s == nc + LAG - 1)
-        def _():
-            for dd in range(1, 8):
-                energy_copy(dd).start()
-
         @pl.when(s >= LAG + 1)
         def _():
             mode_one(s - LAG - 1)
 
         return carry
 
-    mode_three(0)
-    pl.semaphore_wait(barrier, 3)
-    y_copy(0).start()
-    for c in range(1, XBUF):
-        x_copy(c).start()
-    f_copies[1].start()
-    f_copies[2].start()
-    lax.fori_loop(1, nc + LAG + 1, step, 0)
-
-    for dd in (6, 7, 4, 5, 2, 3, 1):
+    first = jnp.zeros((4, 8, 128), F32)
+    for k in range(pieces):
+        x_first[k].wait()
+        if k == 0:
+            for c in range(1, XBUF):
+                x_copy(c).start()
+            f_copies[1].start()
+            f_copies[2].start()
+        first += block(0, 0, k)
+        if k == 0:
+            pl.semaphore_wait(barrier, 3)
+        y_first(k).start()
+    ex[0] = jnp.sum(first, axis=0)
+    x_copy(XBUF).start()
+    lax.fori_loop(1, nc + LAG - 1, step, 0)
+
+    for dd in range(1, 8):
+        energy_copy(dd).start()
+    mode_one(nc - 2)
+    far_first = (6, 7, 4, 5, 2, 3, 1)
+    for dd in far_first:
         last_copy(dd).start()
+    blast[0] = lax.dot_general(u2n[...], mode_two_rows(nc - 1), NT, preferred_element_type=F32)
+    for dd in far_first:
+        wide_copy(dd).start()
     for c in range(nc - RING, nc):
         y_copy(c).wait_send()
-    for c in range(nc - BRING, nc):
+    for c in range(nc - 1 - BRING, nc - 1):
         b_copy(c).wait_send()
+
+    def chip_pair(base):
+        b_here = (blast[base] + blast[base + 2]).astype(BF16)
+        b_twin = (blast[base + 1] + blast[base + 3]).astype(BF16)
+        part = jnp.dot(b_here, w1[nq - 1], preferred_element_type=F32) + jnp.dot(b_twin, w1o[...], preferred_element_type=F32)
+        low, high = part[:8], part[8:]
+        return jnp.where(col == 0, low, high), jnp.where(col == 0, high, low)
+
     last_copy(1).wait()
-    mine = gpart[last] + glast[1]
+    for dd in (1, 2, 3):
+        wide_copy(dd).wait()
+    near = chip_pair(0)
+    mine = (gpart[last] + glast[1]) + near[0]
     grecv[last] = mine
     for b in range(8):
         turned = grecv[:, b, :].T
@@ -226,7 +267,10 @@
     g_energy = tree([energy[dd, 1:] for dd in (0, 2, 4, 6)])
     for dd in range(2, 8):
         last_copy(dd).wait()
-    chips = [mine] + [glast[dd] + glast[dd + 1] for dd in (2, 4, 6)]
+    for dd in range(4, 8):
+        wide_copy(dd).wait()
+    far = chip_pair(4)
+    chips = [mine] + [(glast[dd] + glast[dd + 1]) + add for dd, add in ((2, near[1]), (4, far[0]), (6, far[1]))]
     final = jnp.sum(tree([g * g for g in chips]))
     g_energy = jnp.where(lax.broadcasted_iota(jnp.int32, (1, 128), 1) == last, final, g_energy)
     e_out[...] = ((x_energy - g_energy) / x_energy)[:, :snaps]
@@ -264,7 +308,8 @@
                 pltpu.VMEM((BRING, 8, rows * 8), F32), pltpu.VMEM((BRING, 8, rows * 8), F32), pltpu.VMEM((BRING, 8, rows * 8), F32),
                 pltpu.VMEM((snaps, 8, 128), F32), pltpu.VMEM((snaps, 8, 128), F32),
                 pltpu.VMEM((snaps, 8, 128), F32), pltpu.VMEM((8, 2, 128), F32), pltpu.VMEM((8, 8, 128), F32),
-                dma((XBUF,)), dma((3,)), dma((RING,)), dma((RING,)), dma((BRING,)), dma((BRING,)), dma((2,)), dma((8,)), dma((8,)), dma((8,)), dma((8,)),
+                pltpu.VMEM((16, 128), BF16), pltpu.VMEM((rows * 8, 128), BF16), pltpu.VMEM((8, 16, rows * 8), F32),
+                dma((XBUF,)), dma((3,)), dma((RING,)), dma((RING,)), dma((BRING,)), dma((BRING,)), dma((2,)), dma((8,)), dma((8,)), dma((8,)), dma((8,)), dma((8,)), dma((8,)), dma((rows // SUB,)),
             ],
             compiler_params=pltpu.CompilerParams(collective_id=0, has_side_effects=True, vmem_limit_bytes=40 * 1024 * 1024),
         )(x_block.reshape(nc, rows * 128, 128), *(pltpu.with_memory_space_constraint(f.T, pltpu.HBM) for f in (f_one, f_two, f_three)))

time: 373 us -> 372 us (level)
  no operation moved by 1% of the time
where the time goes in v3:
time: 372 us
  Pallas kernels  371 us (100%)
    pallas_call x1, Pallas kernels, local_part(): pl.pallas_call(functools.partial(kernel, snaps, rows), out_shape=(pltpu.V...  371 us

profile of v3, /device:TPU:0, one launch (start us, length us, event | category | flops | bytes accessed | tf_op | source)
XLA Modules:
  0.0 372.0 jit_solution(5449502427096482747)
XLA Ops:
  0.6 370.7 %shard_map.59 = (f32[8,8,8,32]{3,2,1,0:T(8,128)S(1)}, f32[1,32]{1,0:T(1,128)S(1)}) custom-call(bf16[128,4096,128]{2,1,0:T(8,128)(2,1)} %bitcast.x_hbm, f32[16,256]{1,0:T(8,128)} %bitcast.6, f32[16,256]{1,0:T(8,128)} %bitcast.7, f32[16,256]{1,0:T(8,128)} %bitcast.8), custom_call_target="tpu_custom_call" | custom-call | tf_op jit(solution)/shard_map/pallas_call | solution.py:297
  371.3 0.7 shard_map.60

commit v4 on v3

--- a/solution.py
+++ b/solution.py
@@ -11,10 +11,12 @@
 F32, BF16 = jnp.float32, jnp.bfloat16
 NT = (((1,), (1,)), ((), ()))
 
-LAG = 4
+LAG = 3
 RING = 2 * LAG
+HELD = LAG + 1
 XBUF = 4
 BRING = 4
+BHELD = 2
 SUB = 8
 
 
@@ -38,7 +40,7 @@
 
 def kernel(snaps, rows, x_hbm, f1_hbm, f2_hbm, f3_hbm, g_out, e_out,
            xbuf, f1, f2, f3, u3w, u2w, w1, own, ysend, yrecv, bown, xsend, xrecv,
-           gpart, grecv, ex, energy, glast, u2n, w1o, blast, x_sem, f_sem, ys_sem, yr_sem, xs_sem, xr_sem, g_sem, en_ssem, en_rsem, gl_ssem, gl_rsem, bl_ssem, bl_rsem, x0_sem):
+           gpart, grecv, ex, energy, glast, u2n, w1o, blast, x_sem, ys_sem, yr_sem, xs_sem, xr_sem, g_sem, all_send, all_recv):
     nq = 128 // rows
     nc = snaps * nq
     width = rows * 8
@@ -49,9 +51,9 @@
         slot = lax.rem(c, XBUF)
         return pltpu.make_async_copy(x_hbm.at[c], xbuf.at[slot], x_sem.at[slot])
 
-    f_copies = [pltpu.make_async_copy(src, dst, f_sem.at[k]) for k, (src, dst) in enumerate(((f3_hbm, f3), (f2_hbm, f2), (f1_hbm, f1)))]
+    f_copies = [pltpu.make_async_copy(src, dst, all_send.at[k]) for k, (src, dst) in enumerate(((f3_hbm, f3), (f2_hbm, f2), (f1_hbm, f1)))]
     pieces = rows // SUB
-    x_first = [pltpu.make_async_copy(x_hbm.at[0, pl.ds(k * SUB * 128, SUB * 128)], xbuf.at[0, pl.ds(k * SUB * 128, SUB * 128)], x0_sem.at[k]) for k in range(pieces)]
+    x_first = [pltpu.make_async_copy(x_hbm.at[0, pl.ds(k * SUB * 128, SUB * 128)], xbuf.at[0, pl.ds(k * SUB * 128, SUB * 128)], x_sem.at[k]) for k in range(pieces)]
     x_first[0].start()
     f_copies[0].start()
     for copy in x_first[1:]:
@@ -69,28 +71,32 @@
     ex[...] = jnp.zeros_like(ex)
 
     def y_copy(c):
-        slot = lax.rem(c, RING)
-        return pltpu.make_async_remote_copy(ysend.at[slot], yrecv.at[slot], ys_sem.at[slot], yr_sem.at[slot], device_id=other('slab'), device_id_type=MESH)
+        held, slot = lax.rem(c, HELD), lax.rem(c, RING)
+        return pltpu.make_async_remote_copy(ysend.at[held], yrecv.at[slot], ys_sem.at[lax.rem(c, LAG)], yr_sem.at[slot], device_id=other('slab'), device_id_type=MESH)
 
     def b_copy(c):
-        slot = lax.rem(c, BRING)
-        return pltpu.make_async_remote_copy(xsend.at[slot], xrecv.at[slot], xs_sem.at[slot], xr_sem.at[slot], device_id=other('col'), device_id_type=MESH)
+        held, slot = lax.rem(c, BHELD), lax.rem(c, BRING)
+        return pltpu.make_async_remote_copy(xsend.at[held], xrecv.at[slot], xs_sem.at[held], xr_sem.at[slot], device_id=other('col'), device_id_type=MESH)
 
     def y_first(k):
         part = pl.ds(k * SUB, SUB)
         return pltpu.make_async_remote_copy(ysend.at[0, part], yrecv.at[0, part], ys_sem.at[0], yr_sem.at[0], device_id=other('slab'), device_id_type=MESH)
 
     def wide_copy(dd):
-        return pltpu.make_async_remote_copy(blast.at[0], blast.at[dd], bl_ssem.at[dd], bl_rsem.at[dd], device_id=offset_peer(dd), device_id_type=MESH)
+        return pltpu.make_async_remote_copy(blast.at[0], blast.at[dd], all_send.at[0], all_recv.at[dd // 4], device_id=offset_peer(dd), device_id_type=MESH)
 
     def energy_copy(dd):
-        return pltpu.make_async_remote_copy(energy.at[0], energy.at[dd], en_ssem.at[dd], en_rsem.at[dd], device_id=offset_peer(dd), device_id_type=MESH)
+        return pltpu.make_async_remote_copy(energy.at[0], energy.at[dd], all_send.at[2], all_recv.at[4], device_id=offset_peer(dd), device_id_type=MESH)
 
     def last_copy(dd):
-        return pltpu.make_async_remote_copy(gpart.at[last], glast.at[dd], gl_ssem.at[dd], gl_rsem.at[dd], device_id=offset_peer(dd), device_id_type=MESH)
+        return pltpu.make_async_remote_copy(gpart.at[last], glast.at[dd], all_send.at[1], all_recv.at[2 + dd // 4], device_id=offset_peer(dd), device_id_type=MESH)
+
+    def wait_all(buffer, begin, end, sem):
+        part = buffer.at[pl.ds(begin, end - begin)]
+        pltpu.make_async_copy(part, part, sem).wait()
 
     early = pl.ds(0, last)
-    g_copy = pltpu.make_async_remote_copy(gpart.at[early], grecv.at[early], g_sem.at[0], g_sem.at[1], device_id=other('row'), device_id_type=MESH)
+    g_copy = pltpu.make_async_remote_copy(gpart.at[early], grecv.at[early], all_send.at[2], g_sem.at[0], device_id=other('row'), device_id_type=MESH)
 
     def block(slot, xs, k):
         x = xbuf[xs, pl.ds(pl.multiple_of(k * SUB * 128, SUB * 128), SUB * 128), :]
@@ -102,13 +108,8 @@
         return jnp.sum(xf * xf, axis=0)
 
     def mode_three(c):
-        slot, xs = lax.rem(c, RING), lax.rem(c, XBUF)
+        slot, xs = lax.rem(c, HELD), lax.rem(c, XBUF)
         x_copy(c).wait()
-
-        @pl.when(c >= RING)
-        def _():
-            y_copy(c).wait_send()
-
         acc = lax.fori_loop(0, pieces, lambda k, acc: acc + block(slot, xs, k), jnp.zeros((4, 8, 128), F32))
         t = lax.div(c, nq)
         ex[t] += jnp.sum(acc, axis=0)
@@ -118,14 +119,13 @@
             x_copy(c + XBUF).start()
 
     def mode_two_rows(c):
-        slot = lax.rem(c, RING)
         y_copy(c).wait_recv()
-        return (own[slot] + yrecv[slot]).reshape(width, 128).astype(BF16)
+        return (own[lax.rem(c, HELD)] + yrecv[lax.rem(c, RING)]).reshape(width, 128).astype(BF16)
 
     def mode_two(c):
-        bslot = lax.rem(c, BRING)
-
-        @pl.when(c >= BRING)
+        bslot = lax.rem(c, BHELD)
+
+        @pl.when(c >= BHELD)
         def _():
             b_copy(c).wait_send()
 
@@ -135,9 +135,8 @@
         b_copy(c).start()
 
     def mode_one(c):
-        bslot = lax.rem(c, BRING)
         b_copy(c).wait_recv()
-        b = (bown[bslot] + xrecv[bslot]).astype(BF16)
+        b = (bown[lax.rem(c, BHELD)] + xrecv[lax.rem(c, BRING)]).astype(BF16)
         q, t = lax.rem(c, nq), lax.div(c, nq)
         g = jnp.dot(b, w1[q], preferred_element_type=F32)
 
@@ -178,6 +177,10 @@
         return as_row(jnp.sum(jnp.sum(blocks, axis=1), axis=1, keepdims=True), blocks.shape[0])
 
     def step(s, carry):
+        @pl.when((s > LAG) & (s <= nc))
+        def _():
+            y_copy(s - 1 - LAG).wait_send()
+
         @pl.when((s >= 2) & (s <= nc))
         def _():
             y_copy(s - 1).start()
@@ -219,10 +222,10 @@
     for k in range(pieces):
         x_first[k].wait()
         if k == 0:
-            for c in range(1, XBUF):
-                x_copy(c).start()
             f_copies[1].start()
             f_copies[2].start()
+        else:
+            x_copy(k).start()
         first += block(0, 0, k)
         if k == 0:
             pl.semaphore_wait(barrier, 3)
@@ -240,10 +243,12 @@
     blast[0] = lax.dot_general(u2n[...], mode_two_rows(nc - 1), NT, preferred_element_type=F32)
     for dd in far_first:
         wide_copy(dd).start()
-    for c in range(nc - RING, nc):
+    for c in range(nc - LAG, nc):
         y_copy(c).wait_send()
-    for c in range(nc - 1 - BRING, nc - 1):
+    for c in range(nc - 1 - BHELD, nc - 1):
         b_copy(c).wait_send()
+    wait_all(energy, 1, 8, all_send.at[2])
+    wait_all(glast, 1, 8, all_send.at[1])
 
     def chip_pair(base):
         b_here = (blast[base] + blast[base + 2]).astype(BF16)
@@ -252,23 +257,20 @@
         low, high = part[:8], part[8:]
         return jnp.where(col == 0, low, high), jnp.where(col == 0, high, low)
 
-    last_copy(1).wait()
-    for dd in (1, 2, 3):
-        wide_copy(dd).wait()
+    wait_all(glast, 1, 4, all_recv.at[2])
+    wait_all(blast, 1, 4, all_recv.at[0])
     near = chip_pair(0)
     mine = (gpart[last] + glast[1]) + near[0]
     grecv[last] = mine
     for b in range(8):
         turned = grecv[:, b, :].T
         g_out[:, b] = jnp.where(row == 0, turned[:64], turned[64:]).reshape(8, 8, snaps)
-    for dd in range(1, 8):
-        energy_copy(dd).wait()
+    wait_all(energy, 1, 8, all_recv.at[4])
     x_energy = tree([energy[dd, :1] for dd in range(8)])
     g_energy = tree([energy[dd, 1:] for dd in (0, 2, 4, 6)])
-    for dd in range(2, 8):
-        last_copy(dd).wait()
-    for dd in range(4, 8):
-        wide_copy(dd).wait()
+    wait_all(blast, 1, 8, all_send.at[0])
+    wait_all(glast, 4, 8, all_recv.at[3])
+    wait_all(blast, 4, 8, all_recv.at[1])
     far = chip_pair(4)
     chips = [mine] + [(glast[dd] + glast[dd + 1]) + add for dd, add in ((2, near[1]), (4, far[0]), (6, far[1]))]
     final = jnp.sum(tree([g * g for g in chips]))
@@ -304,12 +306,12 @@
                 pltpu.VMEM((16, 256), F32), pltpu.VMEM((16, 256), F32), pltpu.VMEM((16, 256), F32),
                 pltpu.VMEM((16, 128), BF16), pltpu.VMEM((16, 128), BF16),
                 pltpu.VMEM((nq, rows * 8, 128), BF16),
-                pltpu.VMEM((RING, rows, 8, 128), F32), pltpu.VMEM((RING, rows, 8, 128), F32), pltpu.VMEM((RING, rows, 8, 128), F32),
-                pltpu.VMEM((BRING, 8, rows * 8), F32), pltpu.VMEM((BRING, 8, rows * 8), F32), pltpu.VMEM((BRING, 8, rows * 8), F32),
+                pltpu.VMEM((HELD, rows, 8, 128), F32), pltpu.VMEM((HELD, rows, 8, 128), F32), pltpu.VMEM((RING, rows, 8, 128), F32),
+                pltpu.VMEM((BHELD, 8, rows * 8), F32), pltpu.VMEM((BHELD, 8, rows * 8), F32), pltpu.VMEM((BRING, 8, rows * 8), F32),
                 pltpu.VMEM((snaps, 8, 128), F32), pltpu.VMEM((snaps, 8, 128), F32),
                 pltpu.VMEM((snaps, 8, 128), F32), pltpu.VMEM((8, 2, 128), F32), pltpu.VMEM((8, 8, 128), F32),
                 pltpu.VMEM((16, 128), BF16), pltpu.VMEM((rows * 8, 128), BF16), pltpu.VMEM((8, 16, rows * 8), F32),
-                dma((XBUF,)), dma((3,)), dma((RING,)), dma((RING,)), dma((BRING,)), dma((BRING,)), dma((2,)), dma((8,)), dma((8,)), dma((8,)), dma((8,)), dma((8,)), dma((8,)), dma((rows // SUB,)),
+                dma((XBUF,)), dma((LAG,)), dma((RING,)), dma((BHELD,)), dma((BRING,)), dma((1,)), dma((3,)), dma((5,)),
             ],
             compiler_params=pltpu.CompilerParams(collective_id=0, has_side_effects=True, vmem_limit_bytes=40 * 1024 * 1024),
         )(x_block.reshape(nc, rows * 128, 128), *(pltpu.with_memory_space_constraint(f.T, pltpu.HBM) for f in (f_one, f_two, f_three)))

time: 372 us -> 371 us (level)
  no operation moved by 1% of the time
where the time goes in v4:
time: 371 us
  Pallas kernels  371 us (100%)
    pallas_call x1, Pallas kernels, local_part(): pl.pallas_call(functools.partial(kernel, snaps, rows), out_shape=(pltpu.V...  370 us

profile of v4, /device:TPU:0, one launch (start us, length us, event | category | flops | bytes accessed | tf_op | source)
XLA Modules:
  0.0 371.3 jit_solution(16296512958983401020)
XLA Ops:
  0.6 369.9 %shard_map.59 = (f32[8,8,8,32]{3,2,1,0:T(8,128)S(1)}, f32[1,32]{1,0:T(1,128)S(1)}) custom-call(bf16[128,4096,128]{2,1,0:T(8,128)(2,1)} %bitcast.x_hbm, f32[16,256]{1,0:T(8,128)} %bitcast.6, f32[16,256]{1,0:T(8,128)} %bitcast.7, f32[16,256]{1,0:T(8,128)} %bitcast.8), custom_call_target="tpu_custom_call" | custom-call | tf_op jit(solution)/shard_map/pallas_call | solution.py:299
  370.5 0.7 shard_map.60

commit v5 on v4

--- a/solution.py
+++ b/solution.py
@@ -18,6 +18,7 @@
 BRING = 4
 BHELD = 2
 SUB = 8
+LAST = 2
 
 
 def other(axis):
@@ -40,7 +41,7 @@
 
 def kernel(snaps, rows, x_hbm, f1_hbm, f2_hbm, f3_hbm, g_out, e_out,
            xbuf, f1, f2, f3, u3w, u2w, w1, own, ysend, yrecv, bown, xsend, xrecv,
-           gpart, grecv, ex, energy, glast, u2n, w1o, blast, x_sem, ys_sem, yr_sem, xs_sem, xr_sem, g_sem, all_send, all_recv):
+           gpart, grecv, ex, energy, glast, u2n, w1o, blast, x_sem, ys_sem, yr_sem, xs_sem, xr_sem, g_sem, all_send, all_recv, yls_sem, ylr_sem):
     nq = 128 // rows
     nc = snaps * nq
     width = rows * 8
@@ -82,8 +83,12 @@
         part = pl.ds(k * SUB, SUB)
         return pltpu.make_async_remote_copy(ysend.at[0, part], yrecv.at[0, part], ys_sem.at[0], yr_sem.at[0], device_id=other('slab'), device_id_type=MESH)
 
-    def wide_copy(dd):
-        return pltpu.make_async_remote_copy(blast.at[0], blast.at[dd], all_send.at[0], all_recv.at[dd // 4], device_id=offset_peer(dd), device_id_type=MESH)
+    def y_last(k):
+        part = pl.ds(k * (rows // LAST), rows // LAST)
+        return pltpu.make_async_remote_copy(ysend.at[(nc - 1) % HELD, part], yrecv.at[(nc - 1) % RING, part], yls_sem.at[0], ylr_sem.at[k], device_id=other('slab'), device_id_type=MESH)
+
+    def wide_copy(dd, k):
+        return pltpu.make_async_remote_copy(blast.at[0, k], blast.at[dd, k], all_send.at[0], all_recv.at[dd // 4], device_id=offset_peer(dd), device_id_type=MESH)
 
     def energy_copy(dd):
         return pltpu.make_async_remote_copy(energy.at[0], energy.at[dd], all_send.at[2], all_recv.at[4], device_id=offset_peer(dd), device_id_type=MESH)
@@ -118,10 +123,6 @@
         def _():
             x_copy(c + XBUF).start()
 
-    def mode_two_rows(c):
-        y_copy(c).wait_recv()
-        return (own[lax.rem(c, HELD)] + yrecv[lax.rem(c, RING)]).reshape(width, 128).astype(BF16)
-
     def mode_two(c):
         bslot = lax.rem(c, BHELD)
 
@@ -129,7 +130,9 @@
         def _():
             b_copy(c).wait_send()
 
-        part = lax.dot_general(u2w[...], mode_two_rows(c), NT, preferred_element_type=F32)
+        y_copy(c).wait_recv()
+        a = (own[lax.rem(c, HELD)] + yrecv[lax.rem(c, RING)]).reshape(width, 128).astype(BF16)
+        part = lax.dot_general(u2w[...], a, NT, preferred_element_type=F32)
         bown[bslot] = part[:8]
         xsend[bslot] = part[8:]
         b_copy(c).start()
@@ -181,9 +184,14 @@
         def _():
             y_copy(s - 1 - LAG).wait_send()
 
-        @pl.when((s >= 2) & (s <= nc))
+        @pl.when((s >= 2) & (s < nc))
         def _():
             y_copy(s - 1).start()
+
+        @pl.when(s == nc)
+        def _():
+            for k in range(LAST):
+                y_last(k).start()
 
         @pl.when(s < nc)
         def _():
@@ -236,23 +244,32 @@
 
     for dd in range(1, 8):
         energy_copy(dd).start()
-    mode_one(nc - 2)
     far_first = (6, 7, 4, 5, 2, 3, 1)
-    for dd in far_first:
-        last_copy(dd).start()
-    blast[0] = lax.dot_general(u2n[...], mode_two_rows(nc - 1), NT, preferred_element_type=F32)
-    for dd in far_first:
-        wide_copy(dd).start()
-    for c in range(nc - LAG, nc):
+    for k in range(LAST):
+        if k == LAST - 1:
+            mode_one(nc - 2)
+            for dd in far_first:
+                last_copy(dd).start()
+        y_last(k).wait_recv()
+        part = pl.ds(k * (rows // LAST), rows // LAST)
+        a = (own[(nc - 1) % HELD, part] + yrecv[(nc - 1) % RING, part]).reshape(width // LAST, 128).astype(BF16)
+        blast[0, k] = lax.dot_general(u2n[...], a, NT, preferred_element_type=F32)
+        for dd in far_first:
+            wide_copy(dd, k).start()
+    for c in range(nc - LAG, nc - 1):
         y_copy(c).wait_send()
+    tail = ysend.at[(nc - 1) % HELD]
+    pltpu.make_async_copy(tail, tail, yls_sem.at[0]).wait()
     for c in range(nc - 1 - BHELD, nc - 1):
         b_copy(c).wait_send()
     wait_all(energy, 1, 8, all_send.at[2])
     wait_all(glast, 1, 8, all_send.at[1])
 
     def chip_pair(base):
-        b_here = (blast[base] + blast[base + 2]).astype(BF16)
-        b_twin = (blast[base + 1] + blast[base + 3]).astype(BF16)
+        def summed(first):
+            return jnp.concatenate([blast[first, k] + blast[first + 2, k] for k in range(LAST)], axis=1).astype(BF16)
+
+        b_here, b_twin = summed(base), summed(base + 1)
         part = jnp.dot(b_here, w1[nq - 1], preferred_element_type=F32) + jnp.dot(b_twin, w1o[...], preferred_element_type=F32)
         low, high = part[:8], part[8:]
         return jnp.where(col == 0, low, high), jnp.where(col == 0, high, low)
@@ -310,8 +327,8 @@
                 pltpu.VMEM((BHELD, 8, rows * 8), F32), pltpu.VMEM((BHELD, 8, rows * 8), F32), pltpu.VMEM((BRING, 8, rows * 8), F32),
                 pltpu.VMEM((snaps, 8, 128), F32), pltpu.VMEM((snaps, 8, 128), F32),
                 pltpu.VMEM((snaps, 8, 128), F32), pltpu.VMEM((8, 2, 128), F32), pltpu.VMEM((8, 8, 128), F32),
-                pltpu.VMEM((16, 128), BF16), pltpu.VMEM((rows * 8, 128), BF16), pltpu.VMEM((8, 16, rows * 8), F32),
-                dma((XBUF,)), dma((LAG,)), dma((RING,)), dma((BHELD,)), dma((BRING,)), dma((1,)), dma((3,)), dma((5,)),
+                pltpu.VMEM((16, 128), BF16), pltpu.VMEM((rows * 8, 128), BF16), pltpu.VMEM((8, LAST, 16, rows * 8 // LAST), F32),
+                dma((XBUF,)), dma((LAG,)), dma((RING,)), dma((BHELD,)), dma((BRING,)), dma((1,)), dma((3,)), dma((5,)), dma((1,)), dma((LAST,)),
             ],
             compiler_params=pltpu.CompilerParams(collective_id=0, has_side_effects=True, vmem_limit_bytes=40 * 1024 * 1024),
         )(x_block.reshape(nc, rows * 128, 128), *(pltpu.with_memory_space_constraint(f.T, pltpu.HBM) for f in (f_one, f_two, f_three)))

time: 371 us -> 371 us (level)
  no operation moved by 1% of the time
where the time goes in v5:
time: 371 us
  Pallas kernels  370 us (100%)
    pallas_call x1, Pallas kernels, local_part(): pl.pallas_call(functools.partial(kernel, snaps, rows), out_shape=(pltpu.V...  370 us

profile of v5, /device:TPU:0, one launch (start us, length us, event | category | flops | bytes accessed | tf_op | source)
XLA Modules:
  0.0 371.0 jit_solution(3566310176708176015)
XLA Ops:
  0.6 369.7 %shard_map.59 = (f32[8,8,8,32]{3,2,1,0:T(8,128)S(1)}, f32[1,32]{1,0:T(1,128)S(1)}) custom-call(bf16[128,4096,128]{2,1,0:T(8,128)(2,1)} %bitcast.x_hbm, f32[16,256]{1,0:T(8,128)} %bitcast.6, f32[16,256]{1,0:T(8,128)} %bitcast.7, f32[16,256]{1,0:T(8,128)} %bitcast.8), custom_call_target="tpu_custom_call" | custom-call | tf_op jit(solution)/shard_map/pallas_call | solution.py:316
  370.3 0.7 shard_map.60

commit v6 on v5

--- a/solution.py
+++ b/solution.py
@@ -11,14 +11,14 @@
 F32, BF16 = jnp.float32, jnp.bfloat16
 NT = (((1,), (1,)), ((), ()))
 
-LAG = 3
+LAG = 2
 RING = 2 * LAG
 HELD = LAG + 1
-XBUF = 4
+XBUF = 3
 BRING = 4
 BHELD = 2
 SUB = 8
-LAST = 2
+LAST = 4
 
 
 def other(axis):
@@ -205,20 +205,9 @@
         def _():
             energy[0, :1] = row_sums(ex[...])
 
-        @pl.when(s == nc + LAG - 3)
-        def _():
-            g_copy.start()
-
         @pl.when(s >= LAG)
         def _():
             mode_two(s - LAG)
-
-        @pl.when(s == nc + LAG - 2)
-        def _():
-            g_copy.wait()
-            g = gpart[early] + grecv[early]
-            grecv[early] = g
-            energy[0, 1:] = row_sums(g * g)
 
         @pl.when(s >= LAG + 1)
         def _():
@@ -232,7 +221,7 @@
         if k == 0:
             f_copies[1].start()
             f_copies[2].start()
-        else:
+        elif k < XBUF:
             x_copy(k).start()
         first += block(0, 0, k)
         if k == 0:
@@ -242,8 +231,7 @@
     x_copy(XBUF).start()
     lax.fori_loop(1, nc + LAG - 1, step, 0)
 
-    for dd in range(1, 8):
-        energy_copy(dd).start()
+    g_copy.start()
     far_first = (6, 7, 4, 5, 2, 3, 1)
     for k in range(LAST):
         if k == LAST - 1:
@@ -256,6 +244,13 @@
         blast[0, k] = lax.dot_general(u2n[...], a, NT, preferred_element_type=F32)
         for dd in far_first:
             wide_copy(dd, k).start()
+        if k == 0:
+            g_copy.wait()
+            g = gpart[early] + grecv[early]
+            grecv[early] = g
+            energy[0, 1:] = row_sums(g * g)
+            for dd in range(1, 8):
+                energy_copy(dd).start()
     for c in range(nc - LAG, nc - 1):
         y_copy(c).wait_send()
     tail = ysend.at[(nc - 1) % HELD]
@@ -304,7 +299,7 @@
 
 
 def solution(mesh):
-    rows = 32
+    rows = 64
 
     def local_part(x_block, f_one, f_two, f_three):
         snaps = x_block.shape[0]
@@ -328,7 +323,7 @@
                 pltpu.VMEM((snaps, 8, 128), F32), pltpu.VMEM((snaps, 8, 128), F32),
                 pltpu.VMEM((snaps, 8, 128), F32), pltpu.VMEM((8, 2, 128), F32), pltpu.VMEM((8, 8, 128), F32),
                 pltpu.VMEM((16, 128), BF16), pltpu.VMEM((rows * 8, 128), BF16), pltpu.VMEM((8, LAST, 16, rows * 8 // LAST), F32),
-                dma((XBUF,)), dma((LAG,)), dma((RING,)), dma((BHELD,)), dma((BRING,)), dma((1,)), dma((3,)), dma((5,)), dma((1,)), dma((LAST,)),
+                dma((max(XBUF, rows // SUB),)), dma((LAG,)), dma((RING,)), dma((BHELD,)), dma((BRING,)), dma((1,)), dma((3,)), dma((5,)), dma((1,)), dma((LAST,)),
             ],
             compiler_params=pltpu.CompilerParams(collective_id=0, has_side_effects=True, vmem_limit_bytes=40 * 1024 * 1024),
         )(x_block.reshape(nc, rows * 128, 128), *(pltpu.with_memory_space_constraint(f.T, pltpu.HBM) for f in (f_one, f_two, f_three)))

time: 371 us -> 373 us (level)
  no operation moved by 1% of the time
where the time goes in v6:
time: 373 us
  Pallas kernels  372 us (100%)
    pallas_call x1, Pallas kernels, local_part(): pl.pallas_call(functools.partial(kernel, snaps, rows), out_shape=(pltpu.V...  372 us

profile of v6, /device:TPU:0, one launch (start us, length us, event | category | flops | bytes accessed | tf_op | source)
XLA Modules:
  0.0 373.1 jit_solution(8608740845981969218)
XLA Ops:
  0.6 371.7 %shard_map.59 = (f32[8,8,8,32]{3,2,1,0:T(8,128)S(1)}, f32[1,32]{1,0:T(1,128)S(1)}) custom-call(bf16[64,8192,128]{2,1,0:T(8,128)(2,1)} %bitcast.x_hbm, f32[16,256]{1,0:T(8,128)} %bitcast.6, f32[16,256]{1,0:T(8,128)} %bitcast.7, f32[16,256]{1,0:T(8,128)} %bitcast.8), custom_call_target="tpu_custom_call" | custom-call | tf_op jit(solution)/shard_map/pallas_call | solution.py:311
  372.3 0.7 shard_map.60

commit v7 on v5

--- a/solution.py
+++ b/solution.py
@@ -190,8 +190,14 @@
 
         @pl.when(s == nc)
         def _():
-            for k in range(LAST):
-                y_last(k).start()
+            for c in range(nc - LAG, nc - 2):
+                y_copy(c).wait_send()
+            y_last(0).start()
+
+        @pl.when(s == nc + 1)
+        def _():
+            y_copy(nc - 2).wait_send()
+            y_last(1).start()
 
         @pl.when(s < nc)
         def _():
@@ -256,8 +262,6 @@
         blast[0, k] = lax.dot_general(u2n[...], a, NT, preferred_element_type=F32)
         for dd in far_first:
             wide_copy(dd, k).start()
-    for c in range(nc - LAG, nc - 1):
-        y_copy(c).wait_send()
     tail = ysend.at[(nc - 1) % HELD]
     pltpu.make_async_copy(tail, tail, yls_sem.at[0]).wait()
     for c in range(nc - 1 - BHELD, nc - 1):

time: 371 us -> 371 us (level)
  no operation moved by 1% of the time
where the time goes in v7:
time: 371 us
  Pallas kernels  370 us (100%)
    pallas_call x1, Pallas kernels, local_part(): pl.pallas_call(functools.partial(kernel, snaps, rows), out_shape=(pltpu.V...  370 us

profile of v7, /device:TPU:0, one launch (start us, length us, event | category | flops | bytes accessed | tf_op | source)
XLA Modules:
  0.0 371.0 jit_solution(6419460071844778209)
XLA Ops:
  0.6 369.7 %shard_map.59 = (f32[8,8,8,32]{3,2,1,0:T(8,128)S(1)}, f32[1,32]{1,0:T(1,128)S(1)}) custom-call(bf16[128,4096,128]{2,1,0:T(8,128)(2,1)} %bitcast.x_hbm, f32[16,256]{1,0:T(8,128)} %bitcast.6, f32[16,256]{1,0:T(8,128)} %bitcast.7, f32[16,256]{1,0:T(8,128)} %bitcast.8), custom_call_target="tpu_custom_call" | custom-call | tf_op jit(solution)/shard_map/pallas_call | solution.py:320
  370.3 0.7 shard_map.60

commit v8 on v5

--- a/solution.py
+++ b/solution.py
@@ -11,7 +11,7 @@
 F32, BF16 = jnp.float32, jnp.bfloat16
 NT = (((1,), (1,)), ((), ()))
 
-LAG = 3
+LAG = 5
 RING = 2 * LAG
 HELD = LAG + 1
 XBUF = 4

time: 371 us -> 371 us (level)
  no operation moved by 1% of the time
where the time goes in v8:
time: 371 us
  Pallas kernels  370 us (100%)
    pallas_call x1, Pallas kernels, local_part(): pl.pallas_call(functools.partial(kernel, snaps, rows), out_shape=(pltpu.V...  370 us

profile of v8, /device:TPU:0, one launch (start us, length us, event | category | flops | bytes accessed | tf_op | source)
XLA Modules:
  0.0 371.1 jit_solution(16769352892158891697)
XLA Ops:
  0.6 369.7 %shard_map.59 = (f32[8,8,8,32]{3,2,1,0:T(8,128)S(1)}, f32[1,32]{1,0:T(1,128)S(1)}) custom-call(bf16[128,4096,128]{2,1,0:T(8,128)(2,1)} %bitcast.x_hbm, f32[16,256]{1,0:T(8,128)} %bitcast.6, f32[16,256]{1,0:T(8,128)} %bitcast.7, f32[16,256]{1,0:T(8,128)} %bitcast.8), custom_call_target="tpu_custom_call" | custom-call | tf_op jit(solution)/shard_map/pallas_call | solution.py:316
  370.4 0.7 shard_map.60

commit v9 on v5

--- a/solution.py
+++ b/solution.py
@@ -41,7 +41,7 @@
 
 def kernel(snaps, rows, x_hbm, f1_hbm, f2_hbm, f3_hbm, g_out, e_out,
            xbuf, f1, f2, f3, u3w, u2w, w1, own, ysend, yrecv, bown, xsend, xrecv,
-           gpart, grecv, ex, energy, glast, u2n, w1o, blast, x_sem, ys_sem, yr_sem, xs_sem, xr_sem, g_sem, all_send, all_recv, yls_sem, ylr_sem):
+           gpart, grecv, ex, energy, glast, u2n, w1o, blast, x_sem, ys_sem, yr_sem, xs_sem, xr_sem, g_sem, all_send, all_recv, ylr_sem):
     nq = 128 // rows
     nc = snaps * nq
     width = rows * 8
@@ -85,7 +85,7 @@
 
     def y_last(k):
         part = pl.ds(k * (rows // LAST), rows // LAST)
-        return pltpu.make_async_remote_copy(ysend.at[(nc - 1) % HELD, part], yrecv.at[(nc - 1) % RING, part], yls_sem.at[0], ylr_sem.at[k], device_id=other('slab'), device_id_type=MESH)
+        return pltpu.make_async_remote_copy(ysend.at[(nc - 1) % HELD, part], yrecv.at[(nc - 1) % RING, part], ys_sem.at[(nc - 1) % LAG], yr_sem.at[(nc - 1) % RING] if k == 0 else ylr_sem.at[k - 1], device_id=other('slab'), device_id_type=MESH)
 
     def wide_copy(dd, k):
         return pltpu.make_async_remote_copy(blast.at[0, k], blast.at[dd, k], all_send.at[0], all_recv.at[dd // 4], device_id=offset_peer(dd), device_id_type=MESH)
@@ -256,14 +256,6 @@
         blast[0, k] = lax.dot_general(u2n[...], a, NT, preferred_element_type=F32)
         for dd in far_first:
             wide_copy(dd, k).start()
-    for c in range(nc - LAG, nc - 1):
-        y_copy(c).wait_send()
-    tail = ysend.at[(nc - 1) % HELD]
-    pltpu.make_async_copy(tail, tail, yls_sem.at[0]).wait()
-    for c in range(nc - 1 - BHELD, nc - 1):
-        b_copy(c).wait_send()
-    wait_all(energy, 1, 8, all_send.at[2])
-    wait_all(glast, 1, 8, all_send.at[1])
 
     def chip_pair(base):
         def summed(first):
@@ -285,14 +277,21 @@
     wait_all(energy, 1, 8, all_recv.at[4])
     x_energy = tree([energy[dd, :1] for dd in range(8)])
     g_energy = tree([energy[dd, 1:] for dd in (0, 2, 4, 6)])
-    wait_all(blast, 1, 8, all_send.at[0])
     wait_all(glast, 4, 8, all_recv.at[3])
     wait_all(blast, 4, 8, all_recv.at[1])
     far = chip_pair(4)
     chips = [mine] + [(glast[dd] + glast[dd + 1]) + add for dd, add in ((2, near[1]), (4, far[0]), (6, far[1]))]
-    final = jnp.sum(tree([g * g for g in chips]))
+    final = jnp.sum(jnp.sum(tree([g * g for g in chips]), axis=0, keepdims=True), axis=1, keepdims=True)
     g_energy = jnp.where(lax.broadcasted_iota(jnp.int32, (1, 128), 1) == last, final, g_energy)
     e_out[...] = ((x_energy - g_energy) / x_energy)[:, :snaps]
+
+    for c in range(nc - LAG, nc):
+        y_copy(c).wait_send()
+    for c in range(nc - 1 - BHELD, nc - 1):
+        b_copy(c).wait_send()
+    wait_all(energy, 1, 8, all_send.at[2])
+    wait_all(glast, 1, 8, all_send.at[1])
+    wait_all(blast, 1, 8, all_send.at[0])
 
 
 def finish(g_in, e_in, g_out, e_out, sem):
@@ -328,7 +327,7 @@
                 pltpu.VMEM((snaps, 8, 128), F32), pltpu.VMEM((snaps, 8, 128), F32),
                 pltpu.VMEM((snaps, 8, 128), F32), pltpu.VMEM((8, 2, 128), F32), pltpu.VMEM((8, 8, 128), F32),
                 pltpu.VMEM((16, 128), BF16), pltpu.VMEM((rows * 8, 128), BF16), pltpu.VMEM((8, LAST, 16, rows * 8 // LAST), F32),
-                dma((XBUF,)), dma((LAG,)), dma((RING,)), dma((BHELD,)), dma((BRING,)), dma((1,)), dma((3,)), dma((5,)), dma((1,)), dma((LAST,)),
+                dma((XBUF,)), dma((LAG,)), dma((RING,)), dma((BHELD,)), dma((BRING,)), dma((1,)), dma((3,)), dma((5,)), dma((LAST - 1,)),
             ],
             compiler_params=pltpu.CompilerParams(collective_id=0, has_side_effects=True, vmem_limit_bytes=40 * 1024 * 1024),
         )(x_block.reshape(nc, rows * 128, 128), *(pltpu.with_memory_space_constraint(f.T, pltpu.HBM) for f in (f_one, f_two, f_three)))

time: 371 us -> 371 us (level)
  no operation moved by 1% of the time
where the time goes in v9:
time: 371 us
  Pallas kernels  370 us (100%)
    pallas_call x1, Pallas kernels, local_part(): pl.pallas_call(functools.partial(kernel, snaps, rows), out_shape=(pltpu.V...  370 us

profile of v9, /device:TPU:0, one launch (start us, length us, event | category | flops | bytes accessed | tf_op | source)
XLA Modules:
  0.0 371.0 jit_solution(5960871042782905622)
XLA Ops:
  0.6 369.6 %shard_map.59 = (f32[8,8,8,32]{3,2,1,0:T(8,128)S(1)}, f32[1,32]{1,0:T(1,128)S(1)}) custom-call(bf16[128,4096,128]{2,1,0:T(8,128)(2,1)} %bitcast.x_hbm, f32[16,256]{1,0:T(8,128)} %bitcast.6, f32[16,256]{1,0:T(8,128)} %bitcast.7, f32[16,256]{1,0:T(8,128)} %bitcast.8), custom_call_target="tpu_custom_call" | custom-call | tf_op jit(solution)/shard_map/pallas_call | solution.py:315
  370.3 0.7 shard_map.60

commit v10 on v9

--- a/solution.py
+++ b/solution.py
@@ -87,14 +87,24 @@
         part = pl.ds(k * (rows // LAST), rows // LAST)
         return pltpu.make_async_remote_copy(ysend.at[(nc - 1) % HELD, part], yrecv.at[(nc - 1) % RING, part], ys_sem.at[(nc - 1) % LAG], yr_sem.at[(nc - 1) % RING] if k == 0 else ylr_sem.at[k - 1], device_id=other('slab'), device_id_type=MESH)
 
-    def wide_copy(dd, k):
-        return pltpu.make_async_remote_copy(blast.at[0, k], blast.at[dd, k], all_send.at[0], all_recv.at[dd // 4], device_id=offset_peer(dd), device_id_type=MESH)
-
-    def energy_copy(dd):
-        return pltpu.make_async_remote_copy(energy.at[0], energy.at[dd], all_send.at[2], all_recv.at[4], device_id=offset_peer(dd), device_id_type=MESH)
-
-    def last_copy(dd):
-        return pltpu.make_async_remote_copy(gpart.at[last], glast.at[dd], all_send.at[1], all_recv.at[2 + dd // 4], device_id=offset_peer(dd), device_id_type=MESH)
+    def to_each(send):
+        for dest in range(8):
+            place = {'slab': dest // 4, 'col': dest // 2 % 2, 'row': dest % 2}
+            bits = [lax.axis_index(a) if there == 0 else 1 - lax.axis_index(a) for a, there in place.items()]
+            slot = bits[0] * 4 + bits[1] * 2 + bits[2]
+
+            @pl.when(slot > 0)
+            def _():
+                send(slot, bits[0], place).start()
+
+    def wide_copy(k):
+        return lambda slot, far, place: pltpu.make_async_remote_copy(blast.at[0, k], blast.at[slot, k], all_send.at[0], all_recv.at[far], device_id=place, device_id_type=MESH)
+
+    def energy_copy(slot, far, place):
+        return pltpu.make_async_remote_copy(energy.at[0], energy.at[slot], all_send.at[2], all_recv.at[4], device_id=place, device_id_type=MESH)
+
+    def last_copy(slot, far, place):
+        return pltpu.make_async_remote_copy(gpart.at[last], glast.at[slot], all_send.at[1], all_recv.at[2 + far], device_id=place, device_id_type=MESH)
 
     def wait_all(buffer, begin, end, sem):
         part = buffer.at[pl.ds(begin, end - begin)]
@@ -242,20 +252,16 @@
     x_copy(XBUF).start()
     lax.fori_loop(1, nc + LAG - 1, step, 0)
 
-    for dd in range(1, 8):
-        energy_copy(dd).start()
-    far_first = (6, 7, 4, 5, 2, 3, 1)
+    to_each(energy_copy)
     for k in range(LAST):
         if k == LAST - 1:
             mode_one(nc - 2)
-            for dd in far_first:
-                last_copy(dd).start()
+            to_each(last_copy)
         y_last(k).wait_recv()
         part = pl.ds(k * (rows // LAST), rows // LAST)
         a = (own[(nc - 1) % HELD, part] + yrecv[(nc - 1) % RING, part]).reshape(width // LAST, 128).astype(BF16)
         blast[0, k] = lax.dot_general(u2n[...], a, NT, preferred_element_type=F32)
-        for dd in far_first:
-            wide_copy(dd, k).start()
+        to_each(wide_copy(k))
 
     def chip_pair(base):
         def summed(first):

time: 371 us -> 371 us (level)
  no operation moved by 1% of the time
where the time goes in v10:
time: 371 us
  Pallas kernels  370 us (100%)
    pallas_call x1, Pallas kernels, local_part(): pl.pallas_call(functools.partial(kernel, snaps, rows), out_shape=(pltpu.V...  369 us

profile of v10, /device:TPU:0, one launch (start us, length us, event | category | flops | bytes accessed | tf_op | source)
XLA Modules:
  0.0 370.8 jit_solution(14262015945729424005)
XLA Ops:
  0.6 369.5 %shard_map.59 = (f32[8,8,8,32]{3,2,1,0:T(8,128)S(1)}, f32[1,32]{1,0:T(1,128)S(1)}) custom-call(bf16[128,4096,128]{2,1,0:T(8,128)(2,1)} %bitcast.x_hbm, f32[16,256]{1,0:T(8,128)} %bitcast.6, f32[16,256]{1,0:T(8,128)} %bitcast.7, f32[16,256]{1,0:T(8,128)} %bitcast.8), custom_call_target="tpu_custom_call" | custom-call | tf_op jit(solution)/shard_map/pallas_call | solution.py:321
  370.1 0.7 shard_map.60

commit v11 on v10

--- a/solution.py
+++ b/solution.py
@@ -19,6 +19,7 @@
 BHELD = 2
 SUB = 8
 LAST = 2
+FIRST = (0, 2, 8, 16, 24, 32)
 
 
 def other(axis):
@@ -54,7 +55,11 @@
 
     f_copies = [pltpu.make_async_copy(src, dst, all_send.at[k]) for k, (src, dst) in enumerate(((f3_hbm, f3), (f2_hbm, f2), (f1_hbm, f1)))]
     pieces = rows // SUB
-    x_first = [pltpu.make_async_copy(x_hbm.at[0, pl.ds(k * SUB * 128, SUB * 128)], xbuf.at[0, pl.ds(k * SUB * 128, SUB * 128)], x_sem.at[k]) for k in range(pieces)]
+    spans = list(zip(FIRST[:-1], FIRST[1:]))
+    x_first = []
+    for k, (begin, end) in enumerate(spans):
+        part = pl.ds(begin * 128, (end - begin) * 128)
+        x_first.append(pltpu.make_async_copy(x_hbm.at[0, part], xbuf.at[0, part], x_sem.at[k] if k < XBUF else xs_sem.at[k - XBUF]))
     x_first[0].start()
     f_copies[0].start()
     for copy in x_first[1:]:
@@ -80,7 +85,8 @@
         return pltpu.make_async_remote_copy(xsend.at[held], xrecv.at[slot], xs_sem.at[held], xr_sem.at[slot], device_id=other('col'), device_id_type=MESH)
 
     def y_first(k):
-        part = pl.ds(k * SUB, SUB)
+        begin, end = spans[k]
+        part = pl.ds(begin, end - begin)
         return pltpu.make_async_remote_copy(ysend.at[0, part], yrecv.at[0, part], ys_sem.at[0], yr_sem.at[0], device_id=other('slab'), device_id_type=MESH)
 
     def y_last(k):
@@ -113,19 +119,19 @@
     early = pl.ds(0, last)
     g_copy = pltpu.make_async_remote_copy(gpart.at[early], grecv.at[early], all_send.at[2], g_sem.at[0], device_id=other('row'), device_id_type=MESH)
 
-    def block(slot, xs, k):
-        x = xbuf[xs, pl.ds(pl.multiple_of(k * SUB * 128, SUB * 128), SUB * 128), :]
+    def block(slot, xs, begin, count):
+        x = xbuf[xs, pl.ds(begin * 128, count * 128), :]
         part = lax.dot_general(u3w[...], x, NT, preferred_element_type=F32)
-        for i in range(SUB):
-            own[slot, k * SUB + i] = part[:8, i * 128:(i + 1) * 128]
-            ysend[slot, k * SUB + i] = part[8:, i * 128:(i + 1) * 128]
+        for i in range(count):
+            own[slot, begin + i] = part[:8, i * 128:(i + 1) * 128]
+            ysend[slot, begin + i] = part[8:, i * 128:(i + 1) * 128]
         xf = x.astype(F32).reshape(-1, 4, 8, 128)
         return jnp.sum(xf * xf, axis=0)
 
     def mode_three(c):
         slot, xs = lax.rem(c, HELD), lax.rem(c, XBUF)
         x_copy(c).wait()
-        acc = lax.fori_loop(0, pieces, lambda k, acc: acc + block(slot, xs, k), jnp.zeros((4, 8, 128), F32))
+        acc = lax.fori_loop(0, pieces, lambda k, acc: acc + block(slot, xs, pl.multiple_of(k * SUB, SUB), SUB), jnp.zeros((4, 8, 128), F32))
         t = lax.div(c, nq)
         ex[t] += jnp.sum(acc, axis=0)
 
@@ -237,14 +243,14 @@
         return carry
 
     first = jnp.zeros((4, 8, 128), F32)
-    for k in range(pieces):
+    for k, (begin, end) in enumerate(spans):
         x_first[k].wait()
         if k == 0:
             f_copies[1].start()
             f_copies[2].start()
-        else:
+        elif k < XBUF:
             x_copy(k).start()
-        first += block(0, 0, k)
+        first += block(0, 0, begin, end - begin)
         if k == 0:
             pl.semaphore_wait(barrier, 3)
         y_first(k).start()

time: 371 us -> 371 us (level)
  no operation moved by 1% of the time
where the time goes in v11:
time: 371 us
  Pallas kernels  370 us (100%)
    pallas_call x1, Pallas kernels, local_part(): pl.pallas_call(functools.partial(kernel, snaps, rows), out_shape=(pltpu.V...  370 us

profile of v11, /device:TPU:0, one launch (start us, length us, event | category | flops | bytes accessed | tf_op | source)
XLA Modules:
  0.0 371.0 jit_solution(15830563693828503772)
XLA Ops:
  0.6 369.6 %shard_map.59 = (f32[8,8,8,32]{3,2,1,0:T(8,128)S(1)}, f32[1,32]{1,0:T(1,128)S(1)}) custom-call(bf16[128,4096,128]{2,1,0:T(8,128)(2,1)} %bitcast.x_hbm, f32[16,256]{1,0:T(8,128)} %bitcast.6, f32[16,256]{1,0:T(8,128)} %bitcast.7, f32[16,256]{1,0:T(8,128)} %bitcast.8), custom_call_target="tpu_custom_call" | custom-call | tf_op jit(solution)/shard_map/pallas_call | solution.py:327
  370.3 0.7 shard_map.60

commit v12 on v11

--- a/solution.py
+++ b/solution.py
@@ -14,12 +14,12 @@
 LAG = 3
 RING = 2 * LAG
 HELD = LAG + 1
-XBUF = 4
+XBUF = 2
 BRING = 4
 BHELD = 2
 SUB = 8
 LAST = 2
-FIRST = (0, 2, 8, 16, 24, 32)
+FIRST = (0, 8, 32)
 
 
 def other(axis):

time: 371 us -> 371 us (level)
  no operation moved by 1% of the time
where the time goes in v12:
time: 371 us
  Pallas kernels  370 us (100%)
    pallas_call x1, Pallas kernels, local_part(): pl.pallas_call(functools.partial(kernel, snaps, rows), out_shape=(pltpu.V...  369 us

profile of v12, /device:TPU:0, one launch (start us, length us, event | category | flops | bytes accessed | tf_op | source)
XLA Modules:
  0.0 370.8 jit_solution(13184357585615228455)
XLA Ops:
  0.6 369.4 %shard_map.59 = (f32[8,8,8,32]{3,2,1,0:T(8,128)S(1)}, f32[1,32]{1,0:T(1,128)S(1)}) custom-call(bf16[128,4096,128]{2,1,0:T(8,128)(2,1)} %bitcast.x_hbm, f32[16,256]{1,0:T(8,128)} %bitcast.6, f32[16,256]{1,0:T(8,128)} %bitcast.7, f32[16,256]{1,0:T(8,128)} %bitcast.8), custom_call_target="tpu_custom_call" | custom-call | tf_op jit(solution)/shard_map/pallas_call | solution.py:327
  370.1 0.7 shard_map.60
